TPU v7x, 32 devices: a whole 2x2x4 slice. The times are simulated.
32 devices in a mesh: section: 2 (over x), sht: 16 (over z, y, core).
Axes of the slice: x: 2, y: 2, z: 4, core: 2. Of those that a mesh axis runs over, the one named last changes fastest.
Arguments:
- analysis: bfloat16 [128, 256, 192], P('sht', None, 'section'), may hold values from -6 to 6
- perturbations: bfloat16 [6, 128, 256, 192], P(None, 'sht', None, 'section'), may hold values from -6 to 6
- gain_first: float32 [2, 192], P('section'), may hold values from 0.1 to 1.9
- spectral_gain: float32 [2, 2, 24576], P('section'), may hold values from -6 to 6
- skip_weight: bfloat16 [2, 192, 192], P('section'), may hold values from -0.4375 to 0.4375
- gain_second: float32 [2, 192], P('section'), may hold values from 0.1 to 1.9
- mlp_in: bfloat16 [2, 192, 384], P('section'), may hold values from -0.4375 to 0.4375
- mlp_out: bfloat16 [2, 192, 384], P('section'), may hold values from -0.3125 to 0.3125
Outputs:
- block_outputs: bfloat16 [2, 6, 128, 49152], P('section', None, 'sht')
All inputs are finite; a program needn't handle non-finite values.
Results may differ from a plain program's by a relative error of at most 0.025.
Values may be sent and summed in bfloat16 or wider, within the bound.
A program may use at most 64 MiB of HBM per device.

v0:
```python
import math
import jax
import jax.numpy as jnp
from jax import lax
from jax.sharding import PartitionSpec as P

C = 192
NLAT = 128
NLON = 256
LMAX = 128
MMAX = 128


def shifted_2(value, axis, steps):
    count = lax.axis_size(axis)
    first, last = (max(0, -steps), min(count, count - steps))
    return lax.ppermute(value, axis, [(source, source + steps) for source in range(first, last)])


def legendre_table(nlat, lmax, mmax, nlon, m_first, m_count):
    latitudes = jnp.arange(nlat, dtype=jnp.float32)
    colatitude = math.pi * (latitudes + 0.5) / nlat
    cosine = jnp.cos(colatitude)
    sine = jnp.sin(colatitude)
    orders = jnp.arange(1, mmax, dtype=jnp.float32)
    factors = jnp.cumsum(0.5 * jnp.log((2.0 * orders + 1.0) / (2.0 * orders)))
    log_diag = jnp.concatenate([jnp.zeros((1,), jnp.float32), factors])
    m_index = m_first + jnp.arange(m_count, dtype=jnp.int32)
    picked = jnp.sum(
        jnp.where(
            m_index[:, None] == jnp.arange(mmax, dtype=jnp.int32)[None, :], log_diag[None, :], 0.0
        ),
        axis=1,
    )
    m_float = m_index.astype(jnp.float32)
    diagonal = jnp.exp(picked[None, :] + m_float[None, :] * jnp.log(sine)[:, None]) * math.sqrt(
        0.25 / math.pi
    )
    cos_col = cosine[:, None]

    def advance(carry, degree):
        latest, earlier = carry
        degree_float = degree.astype(jnp.float32)
        lower = jnp.sqrt(
            (4.0 * degree_float * degree_float - 1.0)
            / jnp.maximum(degree_float * degree_float - m_float * m_float, 1.0)
        )
        shifted = degree_float - 1.0
        upper = jnp.sqrt(
            jnp.maximum(shifted * shifted - m_float * m_float, 0.0)
            / jnp.maximum(4.0 * shifted * shifted - 1.0, 1.0)
        )
        recurred = lower[None, :] * (cos_col * latest - upper[None, :] * earlier)
        first_step = jnp.sqrt(2.0 * m_float + 3.0)[None, :] * cos_col * diagonal
        current = jnp.where(
            degree == m_index[None, :],
            diagonal,
            jnp.where(
                degree == m_index[None, :] + 1,
                first_step,
                jnp.where(degree > m_index[None, :] + 1, recurred, 0.0),
            ),
        )
        return ((current, latest), current)

    initial = jnp.zeros((nlat, m_count), jnp.float32)
    _, stacked = lax.scan(advance, (initial, initial), jnp.arange(lmax, dtype=jnp.int32), unroll=8)
    legendre = jnp.transpose(stacked, (1, 0, 2))
    weights = sine * (2.0 * math.pi / nlon) * (math.pi / nlat)
    return (legendre, weights)


def fourier_tables(nlon, mmax):
    samples = jnp.arange(nlon, dtype=jnp.int32)
    orders = jnp.arange(mmax, dtype=jnp.int32)
    phase = (samples[:, None] * orders[None, :] % nlon).astype(jnp.float32) * (2.0 * math.pi / nlon)
    cosines = jnp.cos(phase)
    sines = jnp.sin(phase)
    forward = jnp.stack([cosines, -sines], axis=1).astype(jnp.bfloat16)
    factor = jnp.where(orders == 0, 1.0, 2.0).astype(jnp.float32)
    inverse = jnp.stack([cosines.T * factor[:, None], -sines.T * factor[:, None]], axis=0).astype(
        jnp.bfloat16
    )
    return (forward, inverse)


def layer_norm(values, gain_vector):
    average = jnp.mean(values, axis=-1, keepdims=True)
    centred = values - average
    variance = jnp.mean(centred * centred, axis=-1, keepdims=True)
    return centred * lax.rsqrt(variance + 1e-05) * gain_vector


def apply_gain(coeffs, gain_table):
    real_part = coeffs[:, :, :, 0]
    imag_part = coeffs[:, :, :, 1]
    gain_real = gain_table[0][None, :, None, :]
    gain_imag = gain_table[1][None, :, None, :]
    return jnp.stack(
        [
            real_part * gain_real - imag_part * gain_imag,
            real_part * gain_imag + imag_part * gain_real,
        ],
        axis=3,
    )


def recenter(analysis, perturbations):
    pert_wide = perturbations.astype(jnp.float32)
    average = jnp.mean(pert_wide, axis=0, keepdims=True)
    return (analysis.astype(jnp.float32)[None] + pert_wide - average).astype(jnp.bfloat16)


def project_out(hidden, out_matrix):
    return lax.dot_general(
        hidden, out_matrix, (((1,), (1,)), ((), ())), preferred_element_type=jnp.float32
    )


def per_device(
    analysis, perturbations, gain_first, spectral_gain, skip_weight, gain_second, mlp_in, mlp_out
):
    section_index = lax.axis_index("section")
    section_count = lax.axis_size("section")
    member_count = perturbations.shape[0]
    stacked = jnp.concatenate([analysis[None], perturbations], axis=0)
    gathered = lax.all_gather(stacked, "section", axis=3, tiled=True)
    members = recenter(gathered[0], gathered[1:])
    forward, inverse = fourier_tables(NLON, MMAX)
    full_gain = spectral_gain[0].reshape(2, LMAX, C)
    m_count = MMAX // lax.axis_size("sht")
    legendre, weights = legendre_table(
        NLAT, LMAX, MMAX, NLON, lax.axis_index("sht") * m_count, m_count
    )
    weighted = (legendre * weights[:, None, None]).astype(jnp.bfloat16)
    plain_table = legendre.astype(jnp.bfloat16)

    def spectral(normed):
        batch_rows = normed.shape[0]
        lat_rows = normed.shape[1]
        spectrum = jnp.einsum(
            "bjkc,kpm->bjmpc", normed, forward, preferred_element_type=jnp.float32
        ).astype(jnp.bfloat16)
        spectrum = spectrum.reshape(batch_rows, lat_rows, MMAX, 2 * C)
        exchanged = lax.all_to_all(spectrum, "sht", split_axis=2, concat_axis=1, tiled=True)
        item_count = exchanged.shape[0]
        coeffs = jnp.einsum(
            "jlm,bjmq->blmq", weighted, exchanged, preferred_element_type=jnp.float32
        )
        coeffs = coeffs.reshape(item_count, LMAX, m_count, 2, C)
        filtered = (
            apply_gain(coeffs, full_gain)
            .astype(jnp.bfloat16)
            .reshape(item_count, LMAX, m_count, 2 * C)
        )
        returned = jnp.einsum(
            "jlm,blmq->bjmq", plain_table, filtered, preferred_element_type=jnp.float32
        ).astype(jnp.bfloat16)
        returned = lax.all_to_all(returned, "sht", split_axis=1, concat_axis=2, tiled=True)
        returned = returned.reshape(batch_rows, lat_rows, MMAX, 2, C)
        return jnp.einsum("bjmpc,pmk->bjkc", returned, inverse, preferred_element_type=jnp.float32)

    def sfno_block(current_state):
        state_wide = current_state.astype(jnp.float32)
        channels = current_state.shape[-1]
        normed = layer_norm(state_wide, gain_first[0]).astype(jnp.bfloat16)
        spatial = spectral(normed)
        skipped = jnp.dot(
            normed.reshape(-1, channels), skip_weight[0], preferred_element_type=jnp.float32
        ).reshape(spatial.shape)
        activated = jax.nn.gelu(spatial + skipped, approximate=False)
        second = layer_norm(activated, gain_second[0]).astype(jnp.bfloat16)
        hidden = jax.nn.gelu(
            jnp.dot(second.reshape(-1, channels), mlp_in[0], preferred_element_type=jnp.float32),
            approximate=False,
        ).astype(jnp.bfloat16)
        update = project_out(hidden, mlp_out[0]).reshape(spatial.shape)
        return (state_wide + update).astype(jnp.bfloat16)

    batch_size = 1
    batch_count = member_count // batch_size
    tick_count = section_count + batch_count - 1

    def tick(tick_index, carry):
        current_state, stored = carry
        received = shifted_2(current_state, "section", 1)
        first_rows = lax.dynamic_slice_in_dim(
            members, jnp.minimum(tick_index, batch_count - 1) * batch_size, batch_size, 0
        )
        incoming = jnp.where(section_index == 0, first_rows, received)
        result = sfno_block(incoming)
        position = tick_index - section_index
        is_valid = jnp.logical_and(position >= 0, position < batch_count)
        offset = jnp.clip(position, 0, batch_count - 1) * batch_size
        previous = lax.dynamic_slice_in_dim(stored, offset, batch_size, 0)
        stored = lax.dynamic_update_slice_in_dim(
            stored, jnp.where(is_valid, result, previous), offset, 0
        )
        return (result, stored)

    empty_state = jnp.zeros((batch_size,) + members.shape[1:], jnp.bfloat16)
    _, stored = lax.fori_loop(0, tick_count, tick, (empty_state, jnp.zeros_like(members)))
    merged = stored.reshape(stored.shape[0], stored.shape[1], stored.shape[2] * stored.shape[3])
    return merged[None]


def solution(mesh):
    return jax.shard_map(
        per_device,
        mesh=mesh,
        in_specs=(
            P("sht", None, "section"),
            P(None, "sht", None, "section"),
            P("section", None),
            P("section", None, None),
            P("section", None, None),
            P("section", None),
            P("section", None, None),
            P("section", None, None),
        ),
        out_specs=P("section", None, "sht", None),
        check_vma=False,
    )
```

profile of v0, /device:TPU:11, one launch (start us, length us, event | category | flops | bytes accessed | tf_op | source)
XLA Modules:
  0.0 980.3 jit_solution(16120760669115899107)
XLA Ops:
  10.8 264.0 %while.39 = (s32[]{:T(128)}, f32[128,8]{0,1:T(8,128)S(1)}, f32[128,8]{0,1:T(8,128)S(1)}, f32[16,8,128,8]{2,3,1,0:T(8,128)S(1)}, s32[16,8]{0,1:T(8,128)S(1)}, /*i...) while((s32[]{:T(128)}, f32[128,8]{0,1:T(8,128)S(1)}, ...), condition=%wide.region_4.5_spmd.clone.clone.clone.clone, body=%wide.region_3.4_spmd.clone.clone.clone.clone.sunk | while | flops 102682 | bytes 236492 | solution.py:67
  288.7 666.6 %while.38 = (s32[]{:T(128)}, bf16[1,8,256,192]{2,3,1,0:T(8,128)(2,1)S(1)}, bf16[6,8,256,192]{2,3,1,0:T(8,128)(2,1)}, pred[]{:T(512)}, bf16[6,8,256,192]{2,3,1,0:...) while((s32[]{:T(128)}, ...), condition=%wide.region_10.11_spmd.clone, body=%wide.region_5.10_spmd.clone.sunk | while | flops 1450184704 | bytes 59488172 | solution.py:202
  290.0 19.0 %collective-permute-done = bf16[1,8,256,192]{2,3,1,0:T(8,128)(2,1)S(1)} collective-permute-done((bf16[1,8,256,192]{2,3,1,0:T(8,128)(2,1)S(1)}, bf16[1,8,256,192]{2,3,1,0:T(8,128)(2,1)S(1)}, u32[]{:S(2)}, u32[]{:S(2)}) %collective-permute-start) | collective-permute-done | bytes 786464 | tf_op jit(solution)/shard_map/while/body/eval_jaxpr/ppermute | solution.py:17
  313.4 7.4 all-to-all-start
  320.9 19.6 %all-to-all-done = bf16[1,8,128,384]{3,1,0,2:T(8,128)(2,1)S(1)} async-done(((bf16[1,8,128,384]{3,1,0,2:T(8,128)(2,1)}), bf16[1,8,128,384]{3,1,0,2:T(8,128)(2,1)S(1)}, u32[]{:S(2)}, u32[]{:S(2)}) %all-to-all-start) | async-done | bytes 786464 | tf_op jit(solution)/shard_map/while/body/eval_jaxpr/all_to_all | solution.py:145
  343.2 4.4 all-to-all-start.1
  347.6 19.6 %all-to-all-done.1 = bf16[1,128,8,384]{3,2,0,1:T(8,128)(2,1)S(1)} async-done(((bf16[1,128,8,384]{3,2,0,1:T(8,128)(2,1)}), bf16[1,128,8,384]{3,2,0,1:T(8,128)(2,1)S(1)}, u32[]{:S(2)}, u32[]{:S(2)}) %all-to-all-start.1) | async-done | bytes 786464 | tf_op jit(solution)/shard_map/while/body/eval_jaxpr/all_to_all | solution.py:159
  368.8 4.4 fusion.151
  374.8 7.5 fusion.153
  386.6 20.1 %collective-permute-done = bf16[1,8,256,192]{2,3,1,0:T(8,128)(2,1)S(1)} collective-permute-done((bf16[1,8,256,192]{2,3,1,0:T(8,128)(2,1)S(1)}, bf16[1,8,256,192]{2,3,1,0:T(8,128)(2,1)S(1)}, u32[]{:S(2)}, u32[]{:S(2)}) %collective-permute-start) | collective-permute-done | bytes 786464 | tf_op jit(solution)/shard_map/while/body/eval_jaxpr/ppermute | solution.py:17
  411.1 4.8 all-to-all-start
  415.9 19.6 %all-to-all-done = bf16[1,8,128,384]{3,1,0,2:T(8,128)(2,1)S(1)} async-done(((bf16[1,8,128,384]{3,1,0,2:T(8,128)(2,1)}), bf16[1,8,128,384]{3,1,0,2:T(8,128)(2,1)S(1)}, u32[]{:S(2)}, u32[]{:S(2)}) %all-to-all-start) | async-done | bytes 786464 | tf_op jit(solution)/shard_map/while/body/eval_jaxpr/all_to_all | solution.py:145
  438.2 4.4 all-to-all-start.1
  442.6 19.6 %all-to-all-done.1 = bf16[1,128,8,384]{3,2,0,1:T(8,128)(2,1)S(1)} async-done(((bf16[1,128,8,384]{3,2,0,1:T(8,128)(2,1)}), bf16[1,128,8,384]{3,2,0,1:T(8,128)(2,1)S(1)}, u32[]{:S(2)}, u32[]{:S(2)}) %all-to-all-start.1) | async-done | bytes 786464 | tf_op jit(solution)/shard_map/while/body/eval_jaxpr/all_to_all | solution.py:159
  463.8 4.4 fusion.151
  469.8 7.5 fusion.153
  481.6 20.1 %collective-permute-done = bf16[1,8,256,192]{2,3,1,0:T(8,128)(2,1)S(1)} collective-permute-done((bf16[1,8,256,192]{2,3,1,0:T(8,128)(2,1)S(1)}, bf16[1,8,256,192]{2,3,1,0:T(8,128)(2,1)S(1)}, u32[]{:S(2)}, u32[]{:S(2)}) %collective-permute-start) | collective-permute-done | bytes 786464 | tf_op jit(solution)/shard_map/while/body/eval_jaxpr/ppermute | solution.py:17
  506.1 4.8 all-to-all-start
  510.9 19.6 %all-to-all-done = bf16[1,8,128,384]{3,1,0,2:T(8,128)(2,1)S(1)} async-done(((bf16[1,8,128,384]{3,1,0,2:T(8,128)(2,1)}), bf16[1,8,128,384]{3,1,0,2:T(8,128)(2,1)S(1)}, u32[]{:S(2)}, u32[]{:S(2)}) %all-to-all-start) | async-done | bytes 786464 | tf_op jit(solution)/shard_map/while/body/eval_jaxpr/all_to_all | solution.py:145
  533.2 4.4 all-to-all-start.1
  537.7 19.6 %all-to-all-done.1 = bf16[1,128,8,384]{3,2,0,1:T(8,128)(2,1)S(1)} async-done(((bf16[1,128,8,384]{3,2,0,1:T(8,128)(2,1)}), bf16[1,128,8,384]{3,2,0,1:T(8,128)(2,1)S(1)}, u32[]{:S(2)}, u32[]{:S(2)}) %all-to-all-start.1) | async-done | bytes 786464 | tf_op jit(solution)/shard_map/while/body/eval_jaxpr/all_to_all | solution.py:159
  564.8 7.5 fusion.153
  576.6 20.1 %collective-permute-done = bf16[1,8,256,192]{2,3,1,0:T(8,128)(2,1)S(1)} collective-permute-done((bf16[1,8,256,192]{2,3,1,0:T(8,128)(2,1)S(1)}, bf16[1,8,256,192]{2,3,1,0:T(8,128)(2,1)S(1)}, u32[]{:S(2)}, u32[]{:S(2)}) %collective-permute-start) | collective-permute-done | bytes 786464 | tf_op jit(solution)/shard_map/while/body/eval_jaxpr/ppermute | solution.py:17
  601.1 4.8 all-to-all-start
  605.9 19.6 %all-to-all-done = bf16[1,8,128,384]{3,1,0,2:T(8,128)(2,1)S(1)} async-done(((bf16[1,8,128,384]{3,1,0,2:T(8,128)(2,1)}), bf16[1,8,128,384]{3,1,0,2:T(8,128)(2,1)S(1)}, u32[]{:S(2)}, u32[]{:S(2)}) %all-to-all-start) | async-done | bytes 786464 | tf_op jit(solution)/shard_map/while/body/eval_jaxpr/all_to_all | solution.py:145
  628.2 4.4 all-to-all-start.1
  632.7 19.6 %all-to-all-done.1 = bf16[1,128,8,384]{3,2,0,1:T(8,128)(2,1)S(1)} async-done(((bf16[1,128,8,384]{3,2,0,1:T(8,128)(2,1)}), bf16[1,128,8,384]{3,2,0,1:T(8,128)(2,1)S(1)}, u32[]{:S(2)}, u32[]{:S(2)}) %all-to-all-start.1) | async-done | bytes 786464 | tf_op jit(solution)/shard_map/while/body/eval_jaxpr/all_to_all | solution.py:159
  659.8 7.5 fusion.153
  671.6 20.1 %collective-permute-done = bf16[1,8,256,192]{2,3,1,0:T(8,128)(2,1)S(1)} collective-permute-done((bf16[1,8,256,192]{2,3,1,0:T(8,128)(2,1)S(1)}, bf16[1,8,256,192]{2,3,1,0:T(8,128)(2,1)S(1)}, u32[]{:S(2)}, u32[]{:S(2)}) %collective-permute-start) | collective-permute-done | bytes 786464 | tf_op jit(solution)/shard_map/while/body/eval_jaxpr/ppermute | solution.py:17
  696.1 4.8 all-to-all-start
  700.9 19.6 %all-to-all-done = bf16[1,8,128,384]{3,1,0,2:T(8,128)(2,1)S(1)} async-done(((bf16[1,8,128,384]{3,1,0,2:T(8,128)(2,1)}), bf16[1,8,128,384]{3,1,0,2:T(8,128)(2,1)S(1)}, u32[]{:S(2)}, u32[]{:S(2)}) %all-to-all-start) | async-done | bytes 786464 | tf_op jit(solution)/shard_map/while/body/eval_jaxpr/all_to_all | solution.py:145
  723.2 4.4 all-to-all-start.1
  727.7 19.6 %all-to-all-done.1 = bf16[1,128,8,384]{3,2,0,1:T(8,128)(2,1)S(1)} async-done(((bf16[1,128,8,384]{3,2,0,1:T(8,128)(2,1)}), bf16[1,128,8,384]{3,2,0,1:T(8,128)(2,1)S(1)}, u32[]{:S(2)}, u32[]{:S(2)}) %all-to-all-start.1) | async-done | bytes 786464 | tf_op jit(solution)/shard_map/while/body/eval_jaxpr/all_to_all | solution.py:159
  754.8 7.5 fusion.153
  766.7 20.1 %collective-permute-done = bf16[1,8,256,192]{2,3,1,0:T(8,128)(2,1)S(1)} collective-permute-done((bf16[1,8,256,192]{2,3,1,0:T(8,128)(2,1)S(1)}, bf16[1,8,256,192]{2,3,1,0:T(8,128)(2,1)S(1)}, u32[]{:S(2)}, u32[]{:S(2)}) %collective-permute-start) | collective-permute-done | bytes 786464 | tf_op jit(solution)/shard_map/while/body/eval_jaxpr/ppermute | solution.py:17
  791.1 4.8 all-to-all-start
  795.9 19.6 %all-to-all-done = bf16[1,8,128,384]{3,1,0,2:T(8,128)(2,1)S(1)} async-done(((bf16[1,8,128,384]{3,1,0,2:T(8,128)(2,1)}), bf16[1,8,128,384]{3,1,0,2:T(8,128)(2,1)S(1)}, u32[]{:S(2)}, u32[]{:S(2)}) %all-to-all-start) | async-done | bytes 786464 | tf_op jit(solution)/shard_map/while/body/eval_jaxpr/all_to_all | solution.py:145
  818.2 4.4 all-to-all-start.1
  822.7 19.6 %all-to-all-done.1 = bf16[1,128,8,384]{3,2,0,1:T(8,128)(2,1)S(1)} async-done(((bf16[1,128,8,384]{3,2,0,1:T(8,128)(2,1)}), bf16[1,128,8,384]{3,2,0,1:T(8,128)(2,1)S(1)}, u32[]{:S(2)}, u32[]{:S(2)}) %all-to-all-start.1) | async-done | bytes 786464 | tf_op jit(solution)/shard_map/while/body/eval_jaxpr/all_to_all | solution.py:159
  849.8 7.5 fusion.153
  861.7 20.1 %collective-permute-done = bf16[1,8,256,192]{2,3,1,0:T(8,128)(2,1)S(1)} collective-permute-done((bf16[1,8,256,192]{2,3,1,0:T(8,128)(2,1)S(1)}, bf16[1,8,256,192]{2,3,1,0:T(8,128)(2,1)S(1)}, u32[]{:S(2)}, u32[]{:S(2)}) %collective-permute-start) | collective-permute-done | bytes 786464 | tf_op jit(solution)/shard_map/while/body/eval_jaxpr/ppermute | solution.py:17
  886.1 4.8 all-to-all-start
  890.9 19.6 %all-to-all-done = bf16[1,8,128,384]{3,1,0,2:T(8,128)(2,1)S(1)} async-done(((bf16[1,8,128,384]{3,1,0,2:T(8,128)(2,1)}), bf16[1,8,128,384]{3,1,0,2:T(8,128)(2,1)S(1)}, u32[]{:S(2)}, u32[]{:S(2)}) %all-to-all-start) | async-done | bytes 786464 | tf_op jit(solution)/shard_map/while/body/eval_jaxpr/all_to_all | solution.py:145
  913.3 4.4 all-to-all-start.1
  917.7 19.6 %all-to-all-done.1 = bf16[1,128,8,384]{3,2,0,1:T(8,128)(2,1)S(1)} async-done(((bf16[1,128,8,384]{3,2,0,1:T(8,128)(2,1)}), bf16[1,128,8,384]{3,2,0,1:T(8,128)(2,1)S(1)}, u32[]{:S(2)}, u32[]{:S(2)}) %all-to-all-start.1) | async-done | bytes 786464 | tf_op jit(solution)/shard_map/while/body/eval_jaxpr/all_to_all | solution.py:159
  944.8 7.5 fusion.153
  955.3 8.0 copy.52
  963.2 10.2 %broadcast_in_dim_reshape.3 = bf16[1,6,8,49152]{3,2,1,0:T(8,128)(2,1)} reshape(bf16[6,8,256,192]{3,2,1,0:T(8,128)(2,1)} %copy.52) | data formatting | bytes 9437184 | tf_op jit(solution)/shard_map/broadcast_in_dim;reshape | solution.py:204
  (886 shorter events, 322.2 us)
Async XLA Ops:
  6.5 271.6 %all-gather.2.cloned.1.call-start = ((), (), s32[]{:S(2)}) async-start(), calls=%async_computation.2 | async-start | bytes 8257536 | tf_op jit(solution)/shard_map/all_gather | solution.py:127
  10.7 264.1 %copy-start.9 = (bf16[1,192,192]{2,1,0:T(8,128)(2,1)S(1)}, bf16[1,192,192]{2,1,0:T(8,128)(2,1)}, u32[]{:S(2)}) copy-start(bf16[1,192,192]{2,1,0:T(8,128)(2,1)} %param.16) | copy-start | bytes 221188
  10.8 264.8 %copy-start.8 = (f32[1,2,24576]{2,1,0:T(2,128)S(1)}, f32[1,2,24576]{2,1,0:T(2,128)}, u32[]{:S(2)}) copy-start(f32[1,2,24576]{2,1,0:T(2,128)} %param.15) | copy-start | bytes 589828
  288.7 32.2 %copy-start.5 = (f32[2,128,192]{1,2,0:T(8,128)}, f32[2,128,192]{1,2,0:T(8,128)S(1)}, u32[]{:S(2)}) copy-start(f32[2,128,192]{1,2,0:T(8,128)S(1)} %get-tuple-element.1293) | copy-start | bytes 589828 | tf_op jit(solution)/shard_map/while
  288.7 52.0 %copy-start.3 = (bf16[128,128,8]{1,0,2:T(8,128)(2,1)}, bf16[128,128,8]{1,0,2:T(8,128)(2,1)S(1)}, u32[]{:S(2)}) copy-start(bf16[128,128,8]{1,0,2:T(8,128)(2,1)S(1)} %get-tuple-element.1292) | copy-start | bytes 786436 | tf_op jit(solution)/shard_map/while
  288.7 52.8 %copy-start.1 = (bf16[128,128,8]{1,0,2:T(8,128)(2,1)}, bf16[128,128,8]{1,0,2:T(8,128)(2,1)S(1)}, u32[]{:S(2)}) copy-start(bf16[128,128,8]{1,0,2:T(8,128)(2,1)S(1)} %get-tuple-element.1294) | copy-start | bytes 786436 | tf_op jit(solution)/shard_map/while
  288.7 20.3 %collective-permute-start = (bf16[1,8,256,192]{2,3,1,0:T(8,128)(2,1)S(1)}, bf16[1,8,256,192]{2,3,1,0:T(8,128)(2,1)S(1)}, u32[]{:S(2)}, u32[]{:S(2)}) collective-permute-start(bf16[1,8,256,192]{2,3,1,0:T(8,128)(2,1)S(1)} %broadcast_select_fusion.2), channel_id=1, source_target_pairs={{0,16},{1,17},{2,18},{3,19},{4,20},{5,21},{6,22},{7,23},{8,24},{9,... | collective-permute-start | bytes 2359304 | tf_op jit(solution)/shard_map/while/body/eval_jaxpr/ppermute | solution.py:17
  313.4 27.0 %all-to-all-start = ((bf16[1,8,128,384]{3,1,0,2:T(8,128)(2,1)}), bf16[1,8,128,384]{3,1,0,2:T(8,128)(2,1)S(1)}, u32[]{:S(2)}, u32[]{:S(2)}) async-start(bf16[1,8,128,384]{3,1,0,2:T(8,128)(2,1)} %copy.73), calls=%async_computation | async-start | bytes 1572864 | tf_op jit(solution)/shard_map/while/body/eval_jaxpr/all_to_all | solution.py:145
  343.2 24.1 %all-to-all-start.1 = ((bf16[1,128,8,384]{3,2,0,1:T(8,128)(2,1)}), bf16[1,128,8,384]{3,2,0,1:T(8,128)(2,1)S(1)}, u32[]{:S(2)}, u32[]{:S(2)}) async-start(bf16[1,128,8,384]{3,2,0,1:T(8,128)(2,1)} %copy.76), calls=%async_computation.1 | async-start | bytes 1572864 | tf_op jit(solution)/shard_map/while/body/eval_jaxpr/all_to_all | solution.py:159
  374.8 7.5 copy-start.7
  385.2 30.6 %copy-start.5 = (f32[2,128,192]{1,2,0:T(8,128)}, f32[2,128,192]{1,2,0:T(8,128)S(1)}, u32[]{:S(2)}) copy-start(f32[2,128,192]{1,2,0:T(8,128)S(1)} %get-tuple-element.1293) | copy-start | bytes 589828 | tf_op jit(solution)/shard_map/while
  385.2 50.5 %copy-start.3 = (bf16[128,128,8]{1,0,2:T(8,128)(2,1)}, bf16[128,128,8]{1,0,2:T(8,128)(2,1)S(1)}, u32[]{:S(2)}) copy-start(bf16[128,128,8]{1,0,2:T(8,128)(2,1)S(1)} %get-tuple-element.1292) | copy-start | bytes 786436 | tf_op jit(solution)/shard_map/while
  385.2 51.2 %copy-start.1 = (bf16[128,128,8]{1,0,2:T(8,128)(2,1)}, bf16[128,128,8]{1,0,2:T(8,128)(2,1)S(1)}, u32[]{:S(2)}) copy-start(bf16[128,128,8]{1,0,2:T(8,128)(2,1)S(1)} %get-tuple-element.1294) | copy-start | bytes 786436 | tf_op jit(solution)/shard_map/while
  385.3 21.4 %collective-permute-start = (bf16[1,8,256,192]{2,3,1,0:T(8,128)(2,1)S(1)}, bf16[1,8,256,192]{2,3,1,0:T(8,128)(2,1)S(1)}, u32[]{:S(2)}, u32[]{:S(2)}) collective-permute-start(bf16[1,8,256,192]{2,3,1,0:T(8,128)(2,1)S(1)} %broadcast_select_fusion.2), channel_id=1, source_target_pairs={{0,16},{1,17},{2,18},{3,19},{4,20},{5,21},{6,22},{7,23},{8,24},{9,... | collective-permute-start | bytes 2359304 | tf_op jit(solution)/shard_map/while/body/eval_jaxpr/ppermute | solution.py:17
  411.1 24.4 %all-to-all-start = ((bf16[1,8,128,384]{3,1,0,2:T(8,128)(2,1)}), bf16[1,8,128,384]{3,1,0,2:T(8,128)(2,1)S(1)}, u32[]{:S(2)}, u32[]{:S(2)}) async-start(bf16[1,8,128,384]{3,1,0,2:T(8,128)(2,1)} %copy.73), calls=%async_computation | async-start | bytes 1572864 | tf_op jit(solution)/shard_map/while/body/eval_jaxpr/all_to_all | solution.py:145
  438.2 24.1 %all-to-all-start.1 = ((bf16[1,128,8,384]{3,2,0,1:T(8,128)(2,1)}), bf16[1,128,8,384]{3,2,0,1:T(8,128)(2,1)S(1)}, u32[]{:S(2)}, u32[]{:S(2)}) async-start(bf16[1,128,8,384]{3,2,0,1:T(8,128)(2,1)} %copy.76), calls=%async_computation.1 | async-start | bytes 1572864 | tf_op jit(solution)/shard_map/while/body/eval_jaxpr/all_to_all | solution.py:159
  480.2 30.7 %copy-start.5 = (f32[2,128,192]{1,2,0:T(8,128)}, f32[2,128,192]{1,2,0:T(8,128)S(1)}, u32[]{:S(2)}) copy-start(f32[2,128,192]{1,2,0:T(8,128)S(1)} %get-tuple-element.1293) | copy-start | bytes 589828 | tf_op jit(solution)/shard_map/while
  480.2 50.5 %copy-start.3 = (bf16[128,128,8]{1,0,2:T(8,128)(2,1)}, bf16[128,128,8]{1,0,2:T(8,128)(2,1)S(1)}, u32[]{:S(2)}) copy-start(bf16[128,128,8]{1,0,2:T(8,128)(2,1)S(1)} %get-tuple-element.1292) | copy-start | bytes 786436 | tf_op jit(solution)/shard_map/while
  480.2 51.2 %copy-start.1 = (bf16[128,128,8]{1,0,2:T(8,128)(2,1)}, bf16[128,128,8]{1,0,2:T(8,128)(2,1)S(1)}, u32[]{:S(2)}) copy-start(bf16[128,128,8]{1,0,2:T(8,128)(2,1)S(1)} %get-tuple-element.1294) | copy-start | bytes 786436 | tf_op jit(solution)/shard_map/while
  480.3 21.4 %collective-permute-start = (bf16[1,8,256,192]{2,3,1,0:T(8,128)(2,1)S(1)}, bf16[1,8,256,192]{2,3,1,0:T(8,128)(2,1)S(1)}, u32[]{:S(2)}, u32[]{:S(2)}) collective-permute-start(bf16[1,8,256,192]{2,3,1,0:T(8,128)(2,1)S(1)} %broadcast_select_fusion.2), channel_id=1, source_target_pairs={{0,16},{1,17},{2,18},{3,19},{4,20},{5,21},{6,22},{7,23},{8,24},{9,... | collective-permute-start | bytes 2359304 | tf_op jit(solution)/shard_map/while/body/eval_jaxpr/ppermute | solution.py:17
  506.1 24.4 %all-to-all-start = ((bf16[1,8,128,384]{3,1,0,2:T(8,128)(2,1)}), bf16[1,8,128,384]{3,1,0,2:T(8,128)(2,1)S(1)}, u32[]{:S(2)}, u32[]{:S(2)}) async-start(bf16[1,8,128,384]{3,1,0,2:T(8,128)(2,1)} %copy.73), calls=%async_computation | async-start | bytes 1572864 | tf_op jit(solution)/shard_map/while/body/eval_jaxpr/all_to_all | solution.py:145
  533.2 24.1 %all-to-all-start.1 = ((bf16[1,128,8,384]{3,2,0,1:T(8,128)(2,1)}), bf16[1,128,8,384]{3,2,0,1:T(8,128)(2,1)S(1)}, u32[]{:S(2)}, u32[]{:S(2)}) async-start(bf16[1,128,8,384]{3,2,0,1:T(8,128)(2,1)} %copy.76), calls=%async_computation.1 | async-start | bytes 1572864 | tf_op jit(solution)/shard_map/while/body/eval_jaxpr/all_to_all | solution.py:159
  575.2 30.7 %copy-start.5 = (f32[2,128,192]{1,2,0:T(8,128)}, f32[2,128,192]{1,2,0:T(8,128)S(1)}, u32[]{:S(2)}) copy-start(f32[2,128,192]{1,2,0:T(8,128)S(1)} %get-tuple-element.1293) | copy-start | bytes 589828 | tf_op jit(solution)/shard_map/while
  575.2 50.5 %copy-start.3 = (bf16[128,128,8]{1,0,2:T(8,128)(2,1)}, bf16[128,128,8]{1,0,2:T(8,128)(2,1)S(1)}, u32[]{:S(2)}) copy-start(bf16[128,128,8]{1,0,2:T(8,128)(2,1)S(1)} %get-tuple-element.1292) | copy-start | bytes 786436 | tf_op jit(solution)/shard_map/while
  575.2 51.2 %copy-start.1 = (bf16[128,128,8]{1,0,2:T(8,128)(2,1)}, bf16[128,128,8]{1,0,2:T(8,128)(2,1)S(1)}, u32[]{:S(2)}) copy-start(bf16[128,128,8]{1,0,2:T(8,128)(2,1)S(1)} %get-tuple-element.1294) | copy-start | bytes 786436 | tf_op jit(solution)/shard_map/while
  575.3 21.4 %collective-permute-start = (bf16[1,8,256,192]{2,3,1,0:T(8,128)(2,1)S(1)}, bf16[1,8,256,192]{2,3,1,0:T(8,128)(2,1)S(1)}, u32[]{:S(2)}, u32[]{:S(2)}) collective-permute-start(bf16[1,8,256,192]{2,3,1,0:T(8,128)(2,1)S(1)} %broadcast_select_fusion.2), channel_id=1, source_target_pairs={{0,16},{1,17},{2,18},{3,19},{4,20},{5,21},{6,22},{7,23},{8,24},{9,... | collective-permute-start | bytes 2359304 | tf_op jit(solution)/shard_map/while/body/eval_jaxpr/ppermute | solution.py:17
  601.1 24.4 %all-to-all-start = ((bf16[1,8,128,384]{3,1,0,2:T(8,128)(2,1)}), bf16[1,8,128,384]{3,1,0,2:T(8,128)(2,1)S(1)}, u32[]{:S(2)}, u32[]{:S(2)}) async-start(bf16[1,8,128,384]{3,1,0,2:T(8,128)(2,1)} %copy.73), calls=%async_computation | async-start | bytes 1572864 | tf_op jit(solution)/shard_map/while/body/eval_jaxpr/all_to_all | solution.py:145
  628.2 24.1 %all-to-all-start.1 = ((bf16[1,128,8,384]{3,2,0,1:T(8,128)(2,1)}), bf16[1,128,8,384]{3,2,0,1:T(8,128)(2,1)S(1)}, u32[]{:S(2)}, u32[]{:S(2)}) async-start(bf16[1,128,8,384]{3,2,0,1:T(8,128)(2,1)} %copy.76), calls=%async_computation.1 | async-start | bytes 1572864 | tf_op jit(solution)/shard_map/while/body/eval_jaxpr/all_to_all | solution.py:159
  659.8 7.5 copy-start.7
  670.2 30.7 %copy-start.5 = (f32[2,128,192]{1,2,0:T(8,128)}, f32[2,128,192]{1,2,0:T(8,128)S(1)}, u32[]{:S(2)}) copy-start(f32[2,128,192]{1,2,0:T(8,128)S(1)} %get-tuple-element.1293) | copy-start | bytes 589828 | tf_op jit(solution)/shard_map/while
  670.2 50.5 %copy-start.3 = (bf16[128,128,8]{1,0,2:T(8,128)(2,1)}, bf16[128,128,8]{1,0,2:T(8,128)(2,1)S(1)}, u32[]{:S(2)}) copy-start(bf16[128,128,8]{1,0,2:T(8,128)(2,1)S(1)} %get-tuple-element.1292) | copy-start | bytes 786436 | tf_op jit(solution)/shard_map/while
  670.3 51.2 %copy-start.1 = (bf16[128,128,8]{1,0,2:T(8,128)(2,1)}, bf16[128,128,8]{1,0,2:T(8,128)(2,1)S(1)}, u32[]{:S(2)}) copy-start(bf16[128,128,8]{1,0,2:T(8,128)(2,1)S(1)} %get-tuple-element.1294) | copy-start | bytes 786436 | tf_op jit(solution)/shard_map/while
  670.3 21.4 %collective-permute-start = (bf16[1,8,256,192]{2,3,1,0:T(8,128)(2,1)S(1)}, bf16[1,8,256,192]{2,3,1,0:T(8,128)(2,1)S(1)}, u32[]{:S(2)}, u32[]{:S(2)}) collective-permute-start(bf16[1,8,256,192]{2,3,1,0:T(8,128)(2,1)S(1)} %broadcast_select_fusion.2), channel_id=1, source_target_pairs={{0,16},{1,17},{2,18},{3,19},{4,20},{5,21},{6,22},{7,23},{8,24},{9,... | collective-permute-start | bytes 2359304 | tf_op jit(solution)/shard_map/while/body/eval_jaxpr/ppermute | solution.py:17
  696.1 24.4 %all-to-all-start = ((bf16[1,8,128,384]{3,1,0,2:T(8,128)(2,1)}), bf16[1,8,128,384]{3,1,0,2:T(8,128)(2,1)S(1)}, u32[]{:S(2)}, u32[]{:S(2)}) async-start(bf16[1,8,128,384]{3,1,0,2:T(8,128)(2,1)} %copy.73), calls=%async_computation | async-start | bytes 1572864 | tf_op jit(solution)/shard_map/while/body/eval_jaxpr/all_to_all | solution.py:145
  723.2 24.1 %all-to-all-start.1 = ((bf16[1,128,8,384]{3,2,0,1:T(8,128)(2,1)}), bf16[1,128,8,384]{3,2,0,1:T(8,128)(2,1)S(1)}, u32[]{:S(2)}, u32[]{:S(2)}) async-start(bf16[1,128,8,384]{3,2,0,1:T(8,128)(2,1)} %copy.76), calls=%async_computation.1 | async-start | bytes 1572864 | tf_op jit(solution)/shard_map/while/body/eval_jaxpr/all_to_all | solution.py:159
  754.8 7.5 copy-start.7
  765.2 30.7 %copy-start.5 = (f32[2,128,192]{1,2,0:T(8,128)}, f32[2,128,192]{1,2,0:T(8,128)S(1)}, u32[]{:S(2)}) copy-start(f32[2,128,192]{1,2,0:T(8,128)S(1)} %get-tuple-element.1293) | copy-start | bytes 589828 | tf_op jit(solution)/shard_map/while
  765.3 50.5 %copy-start.3 = (bf16[128,128,8]{1,0,2:T(8,128)(2,1)}, bf16[128,128,8]{1,0,2:T(8,128)(2,1)S(1)}, u32[]{:S(2)}) copy-start(bf16[128,128,8]{1,0,2:T(8,128)(2,1)S(1)} %get-tuple-element.1292) | copy-start | bytes 786436 | tf_op jit(solution)/shard_map/while
  765.3 51.2 %copy-start.1 = (bf16[128,128,8]{1,0,2:T(8,128)(2,1)}, bf16[128,128,8]{1,0,2:T(8,128)(2,1)S(1)}, u32[]{:S(2)}) copy-start(bf16[128,128,8]{1,0,2:T(8,128)(2,1)S(1)} %get-tuple-element.1294) | copy-start | bytes 786436 | tf_op jit(solution)/shard_map/while
  765.3 21.4 %collective-permute-start = (bf16[1,8,256,192]{2,3,1,0:T(8,128)(2,1)S(1)}, bf16[1,8,256,192]{2,3,1,0:T(8,128)(2,1)S(1)}, u32[]{:S(2)}, u32[]{:S(2)}) collective-permute-start(bf16[1,8,256,192]{2,3,1,0:T(8,128)(2,1)S(1)} %broadcast_select_fusion.2), channel_id=1, source_target_pairs={{0,16},{1,17},{2,18},{3,19},{4,20},{5,21},{6,22},{7,23},{8,24},{9,... | collective-permute-start | bytes 2359304 | tf_op jit(solution)/shard_map/while/body/eval_jaxpr/ppermute | solution.py:17
  791.1 24.4 %all-to-all-start = ((bf16[1,8,128,384]{3,1,0,2:T(8,128)(2,1)}), bf16[1,8,128,384]{3,1,0,2:T(8,128)(2,1)S(1)}, u32[]{:S(2)}, u32[]{:S(2)}) async-start(bf16[1,8,128,384]{3,1,0,2:T(8,128)(2,1)} %copy.73), calls=%async_computation | async-start | bytes 1572864 | tf_op jit(solution)/shard_map/while/body/eval_jaxpr/all_to_all | solution.py:145
  818.2 24.1 %all-to-all-start.1 = ((bf16[1,128,8,384]{3,2,0,1:T(8,128)(2,1)}), bf16[1,128,8,384]{3,2,0,1:T(8,128)(2,1)S(1)}, u32[]{:S(2)}, u32[]{:S(2)}) async-start(bf16[1,128,8,384]{3,2,0,1:T(8,128)(2,1)} %copy.76), calls=%async_computation.1 | async-start | bytes 1572864 | tf_op jit(solution)/shard_map/while/body/eval_jaxpr/all_to_all | solution.py:159
  860.3 30.7 %copy-start.5 = (f32[2,128,192]{1,2,0:T(8,128)}, f32[2,128,192]{1,2,0:T(8,128)S(1)}, u32[]{:S(2)}) copy-start(f32[2,128,192]{1,2,0:T(8,128)S(1)} %get-tuple-element.1293) | copy-start | bytes 589828 | tf_op jit(solution)/shard_map/while
  860.3 50.5 %copy-start.3 = (bf16[128,128,8]{1,0,2:T(8,128)(2,1)}, bf16[128,128,8]{1,0,2:T(8,128)(2,1)S(1)}, u32[]{:S(2)}) copy-start(bf16[128,128,8]{1,0,2:T(8,128)(2,1)S(1)} %get-tuple-element.1292) | copy-start | bytes 786436 | tf_op jit(solution)/shard_map/while
  860.3 51.2 %copy-start.1 = (bf16[128,128,8]{1,0,2:T(8,128)(2,1)}, bf16[128,128,8]{1,0,2:T(8,128)(2,1)S(1)}, u32[]{:S(2)}) copy-start(bf16[128,128,8]{1,0,2:T(8,128)(2,1)S(1)} %get-tuple-element.1294) | copy-start | bytes 786436 | tf_op jit(solution)/shard_map/while
  860.4 21.4 %collective-permute-start = (bf16[1,8,256,192]{2,3,1,0:T(8,128)(2,1)S(1)}, bf16[1,8,256,192]{2,3,1,0:T(8,128)(2,1)S(1)}, u32[]{:S(2)}, u32[]{:S(2)}) collective-permute-start(bf16[1,8,256,192]{2,3,1,0:T(8,128)(2,1)S(1)} %broadcast_select_fusion.2), channel_id=1, source_target_pairs={{0,16},{1,17},{2,18},{3,19},{4,20},{5,21},{6,22},{7,23},{8,24},{9,... | collective-permute-start | bytes 2359304 | tf_op jit(solution)/shard_map/while/body/eval_jaxpr/ppermute | solution.py:17
  886.1 24.4 %all-to-all-start = ((bf16[1,8,128,384]{3,1,0,2:T(8,128)(2,1)}), bf16[1,8,128,384]{3,1,0,2:T(8,128)(2,1)S(1)}, u32[]{:S(2)}, u32[]{:S(2)}) async-start(bf16[1,8,128,384]{3,1,0,2:T(8,128)(2,1)} %copy.73), calls=%async_computation | async-start | bytes 1572864 | tf_op jit(solution)/shard_map/while/body/eval_jaxpr/all_to_all | solution.py:145
  913.3 24.1 %all-to-all-start.1 = ((bf16[1,128,8,384]{3,2,0,1:T(8,128)(2,1)}), bf16[1,128,8,384]{3,2,0,1:T(8,128)(2,1)S(1)}, u32[]{:S(2)}, u32[]{:S(2)}) async-start(bf16[1,128,8,384]{3,2,0,1:T(8,128)(2,1)} %copy.76), calls=%async_computation.1 | async-start | bytes 1572864 | tf_op jit(solution)/shard_map/while/body/eval_jaxpr/all_to_all | solution.py:159
  (47 other events, 111.9 us)
Sparse Core Ops, SparseCore 0:
  10.2 71.5 all-gather.1
where the time goes:
time: 987 us; the launch traced here: 980 us
  waiting for transfers between devices  414 us (42%)
  other arithmetic  201 us (20%)
  matrix products  122 us (12%)
  loops' own time  83.8 us (8%)
  starting transfers between devices  76.3 us (8%)
  local copies, waits for them, and re-layouts  69.8 us (7%)
  between operations  13.6 us (1%)
    ppermute x7, waiting for transfers between devices, shifted_2(): lax.ppermute(value, axis, [(source, source + steps) for source in range(f...  140 us
    all_to_all x7, waiting for transfers between devices, spectral(): lax.all_to_all(returned, 'sht', split_axis=1, concat_axis=2, tiled=True)  137 us
    all_to_all x7, waiting for transfers between devices, spectral(): lax.all_to_all(spectrum, 'sht', split_axis=2, concat_axis=1, tiled=True)  137 us
    another operation x1, loops' own time, legendre_table(): lax.scan(advance, (initial, initial), jnp.arange(lmax, dtype=jnp.int32),...  81.8 us
    gt x128, other arithmetic, advance(): degree > m_index[None, :] + 1  78.8 us
    eq x64, other arithmetic, advance(): degree == m_index[None, :]  78.2 us
    dot_general x7, matrix products, sfno_block(): jnp.dot(second.reshape(-1, channels), mlp_in[0], preferred_element_type=j...  52.6 us
    all_to_all x7, starting transfers between devices, spectral(): lax.all_to_all(spectrum, 'sht', split_axis=2, concat_axis=1, tiled=True)  36.1 us
  transfers between devices with their start and end apart: 22, of which 21 were waited for; matrix products, arithmetic and copies ran while one was open for 19% of the time, Pallas kernels for 0%

commit v1 on v0

--- a/solution.py
+++ b/solution.py
@@ -9,6 +9,15 @@
 NLON = 256
 LMAX = 128
 MMAX = 128
+pass_stages_all = lambda shard_in: jnp.concatenate(
+    jax.lax.all_to_all(
+        jnp.stack(jnp.split(shard_in, jax.lax.axis_size("sht"), 2), 0),
+        "sht",
+        concat_axis=0,
+        split_axis=0,
+    ),
+    1,
+)
 
 
 def shifted_2(value, axis, steps):
@@ -142,7 +151,7 @@
             "bjkc,kpm->bjmpc", normed, forward, preferred_element_type=jnp.float32
         ).astype(jnp.bfloat16)
         spectrum = spectrum.reshape(batch_rows, lat_rows, MMAX, 2 * C)
-        exchanged = lax.all_to_all(spectrum, "sht", split_axis=2, concat_axis=1, tiled=True)
+        exchanged = pass_stages_all(spectrum)
         item_count = exchanged.shape[0]
         coeffs = jnp.einsum(
             "jlm,bjmq->blmq", weighted, exchanged, preferred_element_type=jnp.float32

time: 987 us -> 1290 us (1.31)
  local copies, waits for them, and re-layouts: 69.8 us -> 356 us
    while x147 -> x532, local copies, waits for them, and re-layouts: 10.8 us -> 264 us
    split x0 -> x7, local copies, waits for them, and re-layouts: none -> 39 us  [jnp.split(shard_in, jax.lax.axis_size('sht'), 2)]
  transfers between devices with their start and end apart: 22 -> 22, of which waited for: 21 -> 21; matrix products, arithmetic and copies ran while one was open for 19% -> 15% of each run, Pallas kernels for 0% -> 0%
where the time goes in v1:
time: 1290 us; the launch traced here: 1280 us
  waiting for transfers between devices  414 us (32%)
  local copies, waits for them, and re-layouts  356 us (28%)
  other arithmetic  213 us (17%)
  matrix products  117 us (9%)
  loops' own time  87.3 us (7%)
  starting transfers between devices  76.3 us (6%)
  between operations  13.6 us (1%)
    while x532, local copies, waits for them, and re-layouts  264 us
    ppermute x7, waiting for transfers between devices, shifted_2(): lax.ppermute(value, axis, [(source, source + steps) for source in range(f...  140 us
    all_to_all x7, waiting for transfers between devices, spectral(): lax.all_to_all(returned, 'sht', split_axis=1, concat_axis=2, tiled=True)  137 us
    all_to_all x7, waiting for transfers between devices, jax.lax.all_to_all(jnp.stack(jnp.split(shard_in, jax.lax.axis_size('sht')...  137 us
    another operation x1, loops' own time, legendre_table(): lax.scan(advance, (initial, initial), jnp.arange(lmax, dtype=jnp.int32),...  84.9 us
    gt x128, other arithmetic, advance(): degree > m_index[None, :] + 1  81 us
    eq x64, other arithmetic, advance(): degree == m_index[None, :]  80.6 us
    dot_general x7, matrix products, sfno_block(): jnp.dot(second.reshape(-1, channels), mlp_in[0], preferred_element_type=j...  52.6 us
  transfers between devices with their start and end apart: 22, of which 21 were waited for; matrix products, arithmetic and copies ran while one was open for 15% of the time, Pallas kernels for 0%

profile of v1, /device:TPU:11, one launch (start us, length us, event | category | flops | bytes accessed | tf_op | source)
XLA Modules:
  0.0 1277.4 jit_solution(17573320638909009819)
XLA Ops:
  10.8 271.4 %while.39 = (s32[]{:T(128)}, f32[128,8]{0,1:T(8,128)S(1)}, f32[128,8]{0,1:T(8,128)S(1)}, f32[16,8,128,8]{2,3,1,0:T(8,128)S(1)}, s32[16,8]{0,1:T(8,128)S(1)}, /*i...) while((s32[]{:T(128)}, f32[128,8]{0,1:T(8,128)S(1)}, ...), condition=%wide.region_4.5_spmd.clone.clone.clone.clone, body=%wide.region_3.4_spmd.clone.clone.clone.clone.sunk | while | flops 102682 | bytes 236484 | solution.py:76
  297.3 955.0 %while.38 = (s32[]{:T(128)}, bf16[1,8,256,192]{2,3,1,0:T(8,128)(2,1)}, bf16[6,8,256,192]{2,3,1,0:T(8,128)(2,1)}, pred[]{:T(512)}, bf16[6,8,256,192]{2,3,1,0:T(8,...) while((s32[]{:T(128)}, ...), condition=%wide.region_10.11_spmd.clone, body=%wide.region_5.10_spmd.clone.sunk | while | flops 1450184704 | bytes 58836228 | solution.py:211
  298.7 19.0 %collective-permute-done = bf16[1,8,256,192]{2,3,1,0:T(8,128)(2,1)S(1)} collective-permute-done((bf16[1,8,256,192]{2,3,1,0:T(8,128)(2,1)S(1)}, bf16[1,8,256,192]{2,3,1,0:T(8,128)(2,1)S(1)}, u32[]{:S(2)}, u32[]{:S(2)}) %collective-permute-start) | collective-permute-done | bytes 786464 | tf_op jit(solution)/shard_map/while/body/eval_jaxpr/ppermute | solution.py:26
  319.9 5.6 fusion.150
  362.3 7.4 all-to-all-start
  369.8 19.6 %all-to-all-done = bf16[16,1,8,8,384]{4,3,2,1,0:T(8,128)(2,1)S(1)} async-done(((bf16[16,1,8,8,384]{4,3,2,1,0:T(8,128)(2,1)}), bf16[16,1,8,8,384]{4,3,2,1,0:T(8,128)(2,1)S(1)}, u32[]{:S(2)}, u32[]{:S(2)}) %all-to-all-start) | async-done | bytes 786464 | tf_op jit(solution)/shard_map/while/body/eval_jaxpr/all_to_all | solution.py:13
  396.2 19.6 %all-to-all-done.1 = bf16[1,128,8,384]{3,2,0,1:T(8,128)(2,1)S(1)} async-done(((bf16[1,128,8,384]{3,2,0,1:T(8,128)(2,1)}), bf16[1,128,8,384]{3,2,0,1:T(8,128)(2,1)S(1)}, u32[]{:S(2)}, u32[]{:S(2)}) %all-to-all-start.1) | async-done | bytes 786464 | tf_op jit(solution)/shard_map/while/body/eval_jaxpr/all_to_all | solution.py:168
  423.4 7.5 fusion.156
  436.6 20.1 %collective-permute-done = bf16[1,8,256,192]{2,3,1,0:T(8,128)(2,1)S(1)} collective-permute-done((bf16[1,8,256,192]{2,3,1,0:T(8,128)(2,1)S(1)}, bf16[1,8,256,192]{2,3,1,0:T(8,128)(2,1)S(1)}, u32[]{:S(2)}, u32[]{:S(2)}) %collective-permute-start) | collective-permute-done | bytes 786464 | tf_op jit(solution)/shard_map/while/body/eval_jaxpr/ppermute | solution.py:26
  459.0 5.6 fusion.150
  501.3 4.8 all-to-all-start
  506.1 19.6 %all-to-all-done = bf16[16,1,8,8,384]{4,3,2,1,0:T(8,128)(2,1)S(1)} async-done(((bf16[16,1,8,8,384]{4,3,2,1,0:T(8,128)(2,1)}), bf16[16,1,8,8,384]{4,3,2,1,0:T(8,128)(2,1)S(1)}, u32[]{:S(2)}, u32[]{:S(2)}) %all-to-all-start) | async-done | bytes 786464 | tf_op jit(solution)/shard_map/while/body/eval_jaxpr/all_to_all | solution.py:13
  532.6 19.6 %all-to-all-done.1 = bf16[1,128,8,384]{3,2,0,1:T(8,128)(2,1)S(1)} async-done(((bf16[1,128,8,384]{3,2,0,1:T(8,128)(2,1)}), bf16[1,128,8,384]{3,2,0,1:T(8,128)(2,1)S(1)}, u32[]{:S(2)}, u32[]{:S(2)}) %all-to-all-start.1) | async-done | bytes 786464 | tf_op jit(solution)/shard_map/while/body/eval_jaxpr/all_to_all | solution.py:168
  559.8 7.5 fusion.156
  573.0 20.1 %collective-permute-done = bf16[1,8,256,192]{2,3,1,0:T(8,128)(2,1)S(1)} collective-permute-done((bf16[1,8,256,192]{2,3,1,0:T(8,128)(2,1)S(1)}, bf16[1,8,256,192]{2,3,1,0:T(8,128)(2,1)S(1)}, u32[]{:S(2)}, u32[]{:S(2)}) %collective-permute-start) | collective-permute-done | bytes 786464 | tf_op jit(solution)/shard_map/while/body/eval_jaxpr/ppermute | solution.py:26
  595.4 5.6 fusion.150
  637.7 4.8 all-to-all-start
  642.5 19.6 %all-to-all-done = bf16[16,1,8,8,384]{4,3,2,1,0:T(8,128)(2,1)S(1)} async-done(((bf16[16,1,8,8,384]{4,3,2,1,0:T(8,128)(2,1)}), bf16[16,1,8,8,384]{4,3,2,1,0:T(8,128)(2,1)S(1)}, u32[]{:S(2)}, u32[]{:S(2)}) %all-to-all-start) | async-done | bytes 786464 | tf_op jit(solution)/shard_map/while/body/eval_jaxpr/all_to_all | solution.py:13
  669.0 19.6 %all-to-all-done.1 = bf16[1,128,8,384]{3,2,0,1:T(8,128)(2,1)S(1)} async-done(((bf16[1,128,8,384]{3,2,0,1:T(8,128)(2,1)}), bf16[1,128,8,384]{3,2,0,1:T(8,128)(2,1)S(1)}, u32[]{:S(2)}, u32[]{:S(2)}) %all-to-all-start.1) | async-done | bytes 786464 | tf_op jit(solution)/shard_map/while/body/eval_jaxpr/all_to_all | solution.py:168
  696.2 7.5 fusion.156
  709.4 20.1 %collective-permute-done = bf16[1,8,256,192]{2,3,1,0:T(8,128)(2,1)S(1)} collective-permute-done((bf16[1,8,256,192]{2,3,1,0:T(8,128)(2,1)S(1)}, bf16[1,8,256,192]{2,3,1,0:T(8,128)(2,1)S(1)}, u32[]{:S(2)}, u32[]{:S(2)}) %collective-permute-start) | collective-permute-done | bytes 786464 | tf_op jit(solution)/shard_map/while/body/eval_jaxpr/ppermute | solution.py:26
  731.7 5.6 fusion.150
  774.1 4.8 all-to-all-start
  778.9 19.6 %all-to-all-done = bf16[16,1,8,8,384]{4,3,2,1,0:T(8,128)(2,1)S(1)} async-done(((bf16[16,1,8,8,384]{4,3,2,1,0:T(8,128)(2,1)}), bf16[16,1,8,8,384]{4,3,2,1,0:T(8,128)(2,1)S(1)}, u32[]{:S(2)}, u32[]{:S(2)}) %all-to-all-start) | async-done | bytes 786464 | tf_op jit(solution)/shard_map/while/body/eval_jaxpr/all_to_all | solution.py:13
  800.9 4.5 all-to-all-start.1
  805.4 19.6 %all-to-all-done.1 = bf16[1,128,8,384]{3,2,0,1:T(8,128)(2,1)S(1)} async-done(((bf16[1,128,8,384]{3,2,0,1:T(8,128)(2,1)}), bf16[1,128,8,384]{3,2,0,1:T(8,128)(2,1)S(1)}, u32[]{:S(2)}, u32[]{:S(2)}) %all-to-all-start.1) | async-done | bytes 786464 | tf_op jit(solution)/shard_map/while/body/eval_jaxpr/all_to_all | solution.py:168
  832.6 7.5 fusion.156
  845.8 20.1 %collective-permute-done = bf16[1,8,256,192]{2,3,1,0:T(8,128)(2,1)S(1)} collective-permute-done((bf16[1,8,256,192]{2,3,1,0:T(8,128)(2,1)S(1)}, bf16[1,8,256,192]{2,3,1,0:T(8,128)(2,1)S(1)}, u32[]{:S(2)}, u32[]{:S(2)}) %collective-permute-start) | collective-permute-done | bytes 786464 | tf_op jit(solution)/shard_map/while/body/eval_jaxpr/ppermute | solution.py:26
  868.1 5.6 fusion.150
  910.5 4.8 all-to-all-start
  915.3 19.6 %all-to-all-done = bf16[16,1,8,8,384]{4,3,2,1,0:T(8,128)(2,1)S(1)} async-done(((bf16[16,1,8,8,384]{4,3,2,1,0:T(8,128)(2,1)}), bf16[16,1,8,8,384]{4,3,2,1,0:T(8,128)(2,1)S(1)}, u32[]{:S(2)}, u32[]{:S(2)}) %all-to-all-start) | async-done | bytes 786464 | tf_op jit(solution)/shard_map/while/body/eval_jaxpr/all_to_all | solution.py:13
  941.8 19.6 %all-to-all-done.1 = bf16[1,128,8,384]{3,2,0,1:T(8,128)(2,1)S(1)} async-done(((bf16[1,128,8,384]{3,2,0,1:T(8,128)(2,1)}), bf16[1,128,8,384]{3,2,0,1:T(8,128)(2,1)S(1)}, u32[]{:S(2)}, u32[]{:S(2)}) %all-to-all-start.1) | async-done | bytes 786464 | tf_op jit(solution)/shard_map/while/body/eval_jaxpr/all_to_all | solution.py:168
  968.9 7.5 fusion.156
  982.1 20.1 %collective-permute-done = bf16[1,8,256,192]{2,3,1,0:T(8,128)(2,1)S(1)} collective-permute-done((bf16[1,8,256,192]{2,3,1,0:T(8,128)(2,1)S(1)}, bf16[1,8,256,192]{2,3,1,0:T(8,128)(2,1)S(1)}, u32[]{:S(2)}, u32[]{:S(2)}) %collective-permute-start) | collective-permute-done | bytes 786464 | tf_op jit(solution)/shard_map/while/body/eval_jaxpr/ppermute | solution.py:26
  1004.5 5.6 fusion.150
  1046.8 4.8 all-to-all-start
  1051.6 19.6 %all-to-all-done = bf16[16,1,8,8,384]{4,3,2,1,0:T(8,128)(2,1)S(1)} async-done(((bf16[16,1,8,8,384]{4,3,2,1,0:T(8,128)(2,1)}), bf16[16,1,8,8,384]{4,3,2,1,0:T(8,128)(2,1)S(1)}, u32[]{:S(2)}, u32[]{:S(2)}) %all-to-all-start) | async-done | bytes 786464 | tf_op jit(solution)/shard_map/while/body/eval_jaxpr/all_to_all | solution.py:13
  1078.1 19.6 %all-to-all-done.1 = bf16[1,128,8,384]{3,2,0,1:T(8,128)(2,1)S(1)} async-done(((bf16[1,128,8,384]{3,2,0,1:T(8,128)(2,1)}), bf16[1,128,8,384]{3,2,0,1:T(8,128)(2,1)S(1)}, u32[]{:S(2)}, u32[]{:S(2)}) %all-to-all-start.1) | async-done | bytes 786464 | tf_op jit(solution)/shard_map/while/body/eval_jaxpr/all_to_all | solution.py:168
  1105.3 7.5 fusion.156
  1118.5 20.1 %collective-permute-done = bf16[1,8,256,192]{2,3,1,0:T(8,128)(2,1)S(1)} collective-permute-done((bf16[1,8,256,192]{2,3,1,0:T(8,128)(2,1)S(1)}, bf16[1,8,256,192]{2,3,1,0:T(8,128)(2,1)S(1)}, u32[]{:S(2)}, u32[]{:S(2)}) %collective-permute-start) | collective-permute-done | bytes 786464 | tf_op jit(solution)/shard_map/while/body/eval_jaxpr/ppermute | solution.py:26
  1140.9 5.6 fusion.150
  1183.2 4.8 all-to-all-start
  1188.0 19.6 %all-to-all-done = bf16[16,1,8,8,384]{4,3,2,1,0:T(8,128)(2,1)S(1)} async-done(((bf16[16,1,8,8,384]{4,3,2,1,0:T(8,128)(2,1)}), bf16[16,1,8,8,384]{4,3,2,1,0:T(8,128)(2,1)S(1)}, u32[]{:S(2)}, u32[]{:S(2)}) %all-to-all-start) | async-done | bytes 786464 | tf_op jit(solution)/shard_map/while/body/eval_jaxpr/all_to_all | solution.py:13
  1210.1 4.5 all-to-all-start.1
  1214.5 19.6 %all-to-all-done.1 = bf16[1,128,8,384]{3,2,0,1:T(8,128)(2,1)S(1)} async-done(((bf16[1,128,8,384]{3,2,0,1:T(8,128)(2,1)}), bf16[1,128,8,384]{3,2,0,1:T(8,128)(2,1)S(1)}, u32[]{:S(2)}, u32[]{:S(2)}) %all-to-all-start.1) | async-done | bytes 786464 | tf_op jit(solution)/shard_map/while/body/eval_jaxpr/all_to_all | solution.py:168
  1241.7 7.5 fusion.156
  1252.3 8.0 copy.92
  1260.3 10.2 broadcast_in_dim_reshape.3
  (1266 shorter events, 607.8 us)
Async XLA Ops:
  6.5 280.3 %all-gather.2.cloned.1.call-start = ((), (), s32[]{:S(2)}) async-start(), calls=%async_computation.2 | async-start | bytes 8257536 | tf_op jit(solution)/shard_map/all_gather | solution.py:136
  10.7 271.7 %copy-start.17 = (f32[1,2,24576]{2,1,0:T(2,128)S(1)}, f32[1,2,24576]{2,1,0:T(2,128)}, u32[]{:S(2)}) copy-start(f32[1,2,24576]{2,1,0:T(2,128)} %param.15) | copy-start | bytes 589828
  297.3 22.0 %copy-start.18 = (bf16[256,2,128]{2,0,1:T(8,128)(2,1)}, bf16[256,2,128]{2,0,1:T(8,128)(2,1)S(1)}, u32[]{:S(2)}) copy-start(bf16[256,2,128]{2,0,1:T(8,128)(2,1)S(1)} %get-tuple-element.1339) | copy-start | bytes 393220 | tf_op jit(solution)/shard_map/while
  297.4 20.3 %collective-permute-start = (bf16[1,8,256,192]{2,3,1,0:T(8,128)(2,1)S(1)}, bf16[1,8,256,192]{2,3,1,0:T(8,128)(2,1)S(1)}, u32[]{:S(2)}, u32[]{:S(2)}) collective-permute-start(bf16[1,8,256,192]{2,3,1,0:T(8,128)(2,1)S(1)} %broadcast_select_fusion.2), channel_id=1, source_target_pairs={{0,16},{1,17},{2,18},{3,19},{4,20},{5,21},{6,22},{7,23},{8,24},{9,... | collective-permute-start | bytes 2359304 | tf_op jit(solution)/shard_map/while/body/eval_jaxpr/ppermute | solution.py:26
  350.5 8.0 copy-start.3
  351.3 18.5 %copy-start.2 = (f32[2,128,192]{1,2,0:T(8,128)S(1)}, f32[2,128,192]{1,2,0:T(8,128)}, u32[]{:S(2)}) copy-start(f32[2,128,192]{1,2,0:T(8,128)} %get-tuple-element.1341) | copy-start | bytes 589828 | tf_op jit(solution)/shard_map/while
  353.2 36.2 %copy-start.1 = (bf16[128,128,8]{1,0,2:T(8,128)(2,1)S(1)}, bf16[128,128,8]{1,0,2:T(8,128)(2,1)}, u32[]{:S(2)}) copy-start(bf16[128,128,8]{1,0,2:T(8,128)(2,1)} %get-tuple-element.1340) | copy-start | bytes 786436 | tf_op jit(solution)/shard_map/while
  362.3 27.0 %all-to-all-start = ((bf16[16,1,8,8,384]{4,3,2,1,0:T(8,128)(2,1)}), bf16[16,1,8,8,384]{4,3,2,1,0:T(8,128)(2,1)S(1)}, u32[]{:S(2)}, u32[]{:S(2)}) async-start(bf16[16,1,8,8,384]{4,3,2,1,0:T(8,128)(2,1)} %bitcast_dynamic-update-slice_fusion.49), calls=%async_computation | async-start | bytes 1572864 | tf_op jit(solution)/shard_map/while/body/eval_jaxpr/all_to_all | solution.py:13
  391.8 24.1 %all-to-all-start.1 = ((bf16[1,128,8,384]{3,2,0,1:T(8,128)(2,1)}), bf16[1,128,8,384]{3,2,0,1:T(8,128)(2,1)S(1)}, u32[]{:S(2)}, u32[]{:S(2)}) async-start(bf16[1,128,8,384]{3,2,0,1:T(8,128)(2,1)} %copy.156), calls=%async_computation.1 | async-start | bytes 1572864 | tf_op jit(solution)/shard_map/while/body/eval_jaxpr/all_to_all | solution.py:168
  434.1 24.3 %copy-start.18 = (bf16[256,2,128]{2,0,1:T(8,128)(2,1)}, bf16[256,2,128]{2,0,1:T(8,128)(2,1)S(1)}, u32[]{:S(2)}) copy-start(bf16[256,2,128]{2,0,1:T(8,128)(2,1)S(1)} %get-tuple-element.1339) | copy-start | bytes 393220 | tf_op jit(solution)/shard_map/while
  435.3 21.4 %collective-permute-start = (bf16[1,8,256,192]{2,3,1,0:T(8,128)(2,1)S(1)}, bf16[1,8,256,192]{2,3,1,0:T(8,128)(2,1)S(1)}, u32[]{:S(2)}, u32[]{:S(2)}) collective-permute-start(bf16[1,8,256,192]{2,3,1,0:T(8,128)(2,1)S(1)} %broadcast_select_fusion.2), channel_id=1, source_target_pairs={{0,16},{1,17},{2,18},{3,19},{4,20},{5,21},{6,22},{7,23},{8,24},{9,... | collective-permute-start | bytes 2359304 | tf_op jit(solution)/shard_map/while/body/eval_jaxpr/ppermute | solution.py:26
  490.3 15.8 %copy-start.2 = (f32[2,128,192]{1,2,0:T(8,128)S(1)}, f32[2,128,192]{1,2,0:T(8,128)}, u32[]{:S(2)}) copy-start(f32[2,128,192]{1,2,0:T(8,128)} %get-tuple-element.1341) | copy-start | bytes 589828 | tf_op jit(solution)/shard_map/while
  492.2 33.5 %copy-start.1 = (bf16[128,128,8]{1,0,2:T(8,128)(2,1)S(1)}, bf16[128,128,8]{1,0,2:T(8,128)(2,1)}, u32[]{:S(2)}) copy-start(bf16[128,128,8]{1,0,2:T(8,128)(2,1)} %get-tuple-element.1340) | copy-start | bytes 786436 | tf_op jit(solution)/shard_map/while
  501.3 24.4 %all-to-all-start = ((bf16[16,1,8,8,384]{4,3,2,1,0:T(8,128)(2,1)}), bf16[16,1,8,8,384]{4,3,2,1,0:T(8,128)(2,1)S(1)}, u32[]{:S(2)}, u32[]{:S(2)}) async-start(bf16[16,1,8,8,384]{4,3,2,1,0:T(8,128)(2,1)} %bitcast_dynamic-update-slice_fusion.49), calls=%async_computation | async-start | bytes 1572864 | tf_op jit(solution)/shard_map/while/body/eval_jaxpr/all_to_all | solution.py:13
  528.2 24.1 %all-to-all-start.1 = ((bf16[1,128,8,384]{3,2,0,1:T(8,128)(2,1)}), bf16[1,128,8,384]{3,2,0,1:T(8,128)(2,1)S(1)}, u32[]{:S(2)}, u32[]{:S(2)}) async-start(bf16[1,128,8,384]{3,2,0,1:T(8,128)(2,1)} %copy.156), calls=%async_computation.1 | async-start | bytes 1572864 | tf_op jit(solution)/shard_map/while/body/eval_jaxpr/all_to_all | solution.py:168
  570.5 24.3 %copy-start.18 = (bf16[256,2,128]{2,0,1:T(8,128)(2,1)}, bf16[256,2,128]{2,0,1:T(8,128)(2,1)S(1)}, u32[]{:S(2)}) copy-start(bf16[256,2,128]{2,0,1:T(8,128)(2,1)S(1)} %get-tuple-element.1339) | copy-start | bytes 393220 | tf_op jit(solution)/shard_map/while
  571.7 21.4 %collective-permute-start = (bf16[1,8,256,192]{2,3,1,0:T(8,128)(2,1)S(1)}, bf16[1,8,256,192]{2,3,1,0:T(8,128)(2,1)S(1)}, u32[]{:S(2)}, u32[]{:S(2)}) collective-permute-start(bf16[1,8,256,192]{2,3,1,0:T(8,128)(2,1)S(1)} %broadcast_select_fusion.2), channel_id=1, source_target_pairs={{0,16},{1,17},{2,18},{3,19},{4,20},{5,21},{6,22},{7,23},{8,24},{9,... | collective-permute-start | bytes 2359304 | tf_op jit(solution)/shard_map/while/body/eval_jaxpr/ppermute | solution.py:26
  625.9 8.0 copy-start.3
  626.7 15.8 %copy-start.2 = (f32[2,128,192]{1,2,0:T(8,128)S(1)}, f32[2,128,192]{1,2,0:T(8,128)}, u32[]{:S(2)}) copy-start(f32[2,128,192]{1,2,0:T(8,128)} %get-tuple-element.1341) | copy-start | bytes 589828 | tf_op jit(solution)/shard_map/while
  628.6 33.5 %copy-start.1 = (bf16[128,128,8]{1,0,2:T(8,128)(2,1)S(1)}, bf16[128,128,8]{1,0,2:T(8,128)(2,1)}, u32[]{:S(2)}) copy-start(bf16[128,128,8]{1,0,2:T(8,128)(2,1)} %get-tuple-element.1340) | copy-start | bytes 786436 | tf_op jit(solution)/shard_map/while
  637.7 24.4 %all-to-all-start = ((bf16[16,1,8,8,384]{4,3,2,1,0:T(8,128)(2,1)}), bf16[16,1,8,8,384]{4,3,2,1,0:T(8,128)(2,1)S(1)}, u32[]{:S(2)}, u32[]{:S(2)}) async-start(bf16[16,1,8,8,384]{4,3,2,1,0:T(8,128)(2,1)} %bitcast_dynamic-update-slice_fusion.49), calls=%async_computation | async-start | bytes 1572864 | tf_op jit(solution)/shard_map/while/body/eval_jaxpr/all_to_all | solution.py:13
  664.6 24.1 %all-to-all-start.1 = ((bf16[1,128,8,384]{3,2,0,1:T(8,128)(2,1)}), bf16[1,128,8,384]{3,2,0,1:T(8,128)(2,1)S(1)}, u32[]{:S(2)}, u32[]{:S(2)}) async-start(bf16[1,128,8,384]{3,2,0,1:T(8,128)(2,1)} %copy.156), calls=%async_computation.1 | async-start | bytes 1572864 | tf_op jit(solution)/shard_map/while/body/eval_jaxpr/all_to_all | solution.py:168
  706.8 24.3 %copy-start.18 = (bf16[256,2,128]{2,0,1:T(8,128)(2,1)}, bf16[256,2,128]{2,0,1:T(8,128)(2,1)S(1)}, u32[]{:S(2)}) copy-start(bf16[256,2,128]{2,0,1:T(8,128)(2,1)S(1)} %get-tuple-element.1339) | copy-start | bytes 393220 | tf_op jit(solution)/shard_map/while
  708.1 21.4 %collective-permute-start = (bf16[1,8,256,192]{2,3,1,0:T(8,128)(2,1)S(1)}, bf16[1,8,256,192]{2,3,1,0:T(8,128)(2,1)S(1)}, u32[]{:S(2)}, u32[]{:S(2)}) collective-permute-start(bf16[1,8,256,192]{2,3,1,0:T(8,128)(2,1)S(1)} %broadcast_select_fusion.2), channel_id=1, source_target_pairs={{0,16},{1,17},{2,18},{3,19},{4,20},{5,21},{6,22},{7,23},{8,24},{9,... | collective-permute-start | bytes 2359304 | tf_op jit(solution)/shard_map/while/body/eval_jaxpr/ppermute | solution.py:26
  762.3 8.0 copy-start.3
  763.1 15.8 %copy-start.2 = (f32[2,128,192]{1,2,0:T(8,128)S(1)}, f32[2,128,192]{1,2,0:T(8,128)}, u32[]{:S(2)}) copy-start(f32[2,128,192]{1,2,0:T(8,128)} %get-tuple-element.1341) | copy-start | bytes 589828 | tf_op jit(solution)/shard_map/while
  764.9 33.5 %copy-start.1 = (bf16[128,128,8]{1,0,2:T(8,128)(2,1)S(1)}, bf16[128,128,8]{1,0,2:T(8,128)(2,1)}, u32[]{:S(2)}) copy-start(bf16[128,128,8]{1,0,2:T(8,128)(2,1)} %get-tuple-element.1340) | copy-start | bytes 786436 | tf_op jit(solution)/shard_map/while
  774.1 24.4 %all-to-all-start = ((bf16[16,1,8,8,384]{4,3,2,1,0:T(8,128)(2,1)}), bf16[16,1,8,8,384]{4,3,2,1,0:T(8,128)(2,1)S(1)}, u32[]{:S(2)}, u32[]{:S(2)}) async-start(bf16[16,1,8,8,384]{4,3,2,1,0:T(8,128)(2,1)} %bitcast_dynamic-update-slice_fusion.49), calls=%async_computation | async-start | bytes 1572864 | tf_op jit(solution)/shard_map/while/body/eval_jaxpr/all_to_all | solution.py:13
  800.9 24.1 %all-to-all-start.1 = ((bf16[1,128,8,384]{3,2,0,1:T(8,128)(2,1)}), bf16[1,128,8,384]{3,2,0,1:T(8,128)(2,1)S(1)}, u32[]{:S(2)}, u32[]{:S(2)}) async-start(bf16[1,128,8,384]{3,2,0,1:T(8,128)(2,1)} %copy.156), calls=%async_computation.1 | async-start | bytes 1572864 | tf_op jit(solution)/shard_map/while/body/eval_jaxpr/all_to_all | solution.py:168
  843.2 24.3 %copy-start.18 = (bf16[256,2,128]{2,0,1:T(8,128)(2,1)}, bf16[256,2,128]{2,0,1:T(8,128)(2,1)S(1)}, u32[]{:S(2)}) copy-start(bf16[256,2,128]{2,0,1:T(8,128)(2,1)S(1)} %get-tuple-element.1339) | copy-start | bytes 393220 | tf_op jit(solution)/shard_map/while
  844.5 21.4 %collective-permute-start = (bf16[1,8,256,192]{2,3,1,0:T(8,128)(2,1)S(1)}, bf16[1,8,256,192]{2,3,1,0:T(8,128)(2,1)S(1)}, u32[]{:S(2)}, u32[]{:S(2)}) collective-permute-start(bf16[1,8,256,192]{2,3,1,0:T(8,128)(2,1)S(1)} %broadcast_select_fusion.2), channel_id=1, source_target_pairs={{0,16},{1,17},{2,18},{3,19},{4,20},{5,21},{6,22},{7,23},{8,24},{9,... | collective-permute-start | bytes 2359304 | tf_op jit(solution)/shard_map/while/body/eval_jaxpr/ppermute | solution.py:26
  899.4 15.8 %copy-start.2 = (f32[2,128,192]{1,2,0:T(8,128)S(1)}, f32[2,128,192]{1,2,0:T(8,128)}, u32[]{:S(2)}) copy-start(f32[2,128,192]{1,2,0:T(8,128)} %get-tuple-element.1341) | copy-start | bytes 589828 | tf_op jit(solution)/shard_map/while
  901.3 33.5 %copy-start.1 = (bf16[128,128,8]{1,0,2:T(8,128)(2,1)S(1)}, bf16[128,128,8]{1,0,2:T(8,128)(2,1)}, u32[]{:S(2)}) copy-start(bf16[128,128,8]{1,0,2:T(8,128)(2,1)} %get-tuple-element.1340) | copy-start | bytes 786436 | tf_op jit(solution)/shard_map/while
  910.5 24.4 %all-to-all-start = ((bf16[16,1,8,8,384]{4,3,2,1,0:T(8,128)(2,1)}), bf16[16,1,8,8,384]{4,3,2,1,0:T(8,128)(2,1)S(1)}, u32[]{:S(2)}, u32[]{:S(2)}) async-start(bf16[16,1,8,8,384]{4,3,2,1,0:T(8,128)(2,1)} %bitcast_dynamic-update-slice_fusion.49), calls=%async_computation | async-start | bytes 1572864 | tf_op jit(solution)/shard_map/while/body/eval_jaxpr/all_to_all | solution.py:13
  937.3 24.1 %all-to-all-start.1 = ((bf16[1,128,8,384]{3,2,0,1:T(8,128)(2,1)}), bf16[1,128,8,384]{3,2,0,1:T(8,128)(2,1)S(1)}, u32[]{:S(2)}, u32[]{:S(2)}) async-start(bf16[1,128,8,384]{3,2,0,1:T(8,128)(2,1)} %copy.156), calls=%async_computation.1 | async-start | bytes 1572864 | tf_op jit(solution)/shard_map/while/body/eval_jaxpr/all_to_all | solution.py:168
  979.6 24.3 %copy-start.18 = (bf16[256,2,128]{2,0,1:T(8,128)(2,1)}, bf16[256,2,128]{2,0,1:T(8,128)(2,1)S(1)}, u32[]{:S(2)}) copy-start(bf16[256,2,128]{2,0,1:T(8,128)(2,1)S(1)} %get-tuple-element.1339) | copy-start | bytes 393220 | tf_op jit(solution)/shard_map/while
  980.8 21.4 %collective-permute-start = (bf16[1,8,256,192]{2,3,1,0:T(8,128)(2,1)S(1)}, bf16[1,8,256,192]{2,3,1,0:T(8,128)(2,1)S(1)}, u32[]{:S(2)}, u32[]{:S(2)}) collective-permute-start(bf16[1,8,256,192]{2,3,1,0:T(8,128)(2,1)S(1)} %broadcast_select_fusion.2), channel_id=1, source_target_pairs={{0,16},{1,17},{2,18},{3,19},{4,20},{5,21},{6,22},{7,23},{8,24},{9,... | collective-permute-start | bytes 2359304 | tf_op jit(solution)/shard_map/while/body/eval_jaxpr/ppermute | solution.py:26
  1035.1 8.0 copy-start.3
  1035.8 15.8 %copy-start.2 = (f32[2,128,192]{1,2,0:T(8,128)S(1)}, f32[2,128,192]{1,2,0:T(8,128)}, u32[]{:S(2)}) copy-start(f32[2,128,192]{1,2,0:T(8,128)} %get-tuple-element.1341) | copy-start | bytes 589828 | tf_op jit(solution)/shard_map/while
  1037.7 33.5 %copy-start.1 = (bf16[128,128,8]{1,0,2:T(8,128)(2,1)S(1)}, bf16[128,128,8]{1,0,2:T(8,128)(2,1)}, u32[]{:S(2)}) copy-start(bf16[128,128,8]{1,0,2:T(8,128)(2,1)} %get-tuple-element.1340) | copy-start | bytes 786436 | tf_op jit(solution)/shard_map/while
  1046.8 24.4 %all-to-all-start = ((bf16[16,1,8,8,384]{4,3,2,1,0:T(8,128)(2,1)}), bf16[16,1,8,8,384]{4,3,2,1,0:T(8,128)(2,1)S(1)}, u32[]{:S(2)}, u32[]{:S(2)}) async-start(bf16[16,1,8,8,384]{4,3,2,1,0:T(8,128)(2,1)} %bitcast_dynamic-update-slice_fusion.49), calls=%async_computation | async-start | bytes 1572864 | tf_op jit(solution)/shard_map/while/body/eval_jaxpr/all_to_all | solution.py:13
  1073.7 24.1 %all-to-all-start.1 = ((bf16[1,128,8,384]{3,2,0,1:T(8,128)(2,1)}), bf16[1,128,8,384]{3,2,0,1:T(8,128)(2,1)S(1)}, u32[]{:S(2)}, u32[]{:S(2)}) async-start(bf16[1,128,8,384]{3,2,0,1:T(8,128)(2,1)} %copy.156), calls=%async_computation.1 | async-start | bytes 1572864 | tf_op jit(solution)/shard_map/while/body/eval_jaxpr/all_to_all | solution.py:168
  1116.0 24.3 %copy-start.18 = (bf16[256,2,128]{2,0,1:T(8,128)(2,1)}, bf16[256,2,128]{2,0,1:T(8,128)(2,1)S(1)}, u32[]{:S(2)}) copy-start(bf16[256,2,128]{2,0,1:T(8,128)(2,1)S(1)} %get-tuple-element.1339) | copy-start | bytes 393220 | tf_op jit(solution)/shard_map/while
  1117.2 21.4 %collective-permute-start = (bf16[1,8,256,192]{2,3,1,0:T(8,128)(2,1)S(1)}, bf16[1,8,256,192]{2,3,1,0:T(8,128)(2,1)S(1)}, u32[]{:S(2)}, u32[]{:S(2)}) collective-permute-start(bf16[1,8,256,192]{2,3,1,0:T(8,128)(2,1)S(1)} %broadcast_select_fusion.2), channel_id=1, source_target_pairs={{0,16},{1,17},{2,18},{3,19},{4,20},{5,21},{6,22},{7,23},{8,24},{9,... | collective-permute-start | bytes 2359304 | tf_op jit(solution)/shard_map/while/body/eval_jaxpr/ppermute | solution.py:26
  1172.2 15.8 %copy-start.2 = (f32[2,128,192]{1,2,0:T(8,128)S(1)}, f32[2,128,192]{1,2,0:T(8,128)}, u32[]{:S(2)}) copy-start(f32[2,128,192]{1,2,0:T(8,128)} %get-tuple-element.1341) | copy-start | bytes 589828 | tf_op jit(solution)/shard_map/while
  1174.1 33.5 %copy-start.1 = (bf16[128,128,8]{1,0,2:T(8,128)(2,1)S(1)}, bf16[128,128,8]{1,0,2:T(8,128)(2,1)}, u32[]{:S(2)}) copy-start(bf16[128,128,8]{1,0,2:T(8,128)(2,1)} %get-tuple-element.1340) | copy-start | bytes 786436 | tf_op jit(solution)/shard_map/while
  1183.2 24.4 %all-to-all-start = ((bf16[16,1,8,8,384]{4,3,2,1,0:T(8,128)(2,1)}), bf16[16,1,8,8,384]{4,3,2,1,0:T(8,128)(2,1)S(1)}, u32[]{:S(2)}, u32[]{:S(2)}) async-start(bf16[16,1,8,8,384]{4,3,2,1,0:T(8,128)(2,1)} %bitcast_dynamic-update-slice_fusion.49), calls=%async_computation | async-start | bytes 1572864 | tf_op jit(solution)/shard_map/while/body/eval_jaxpr/all_to_all | solution.py:13
  1210.1 24.1 %all-to-all-start.1 = ((bf16[1,128,8,384]{3,2,0,1:T(8,128)(2,1)}), bf16[1,128,8,384]{3,2,0,1:T(8,128)(2,1)S(1)}, u32[]{:S(2)}, u32[]{:S(2)}) async-start(bf16[1,128,8,384]{3,2,0,1:T(8,128)(2,1)} %copy.156), calls=%async_computation.1 | async-start | bytes 1572864 | tf_op jit(solution)/shard_map/while/body/eval_jaxpr/all_to_all | solution.py:168
  (132 other events, 384.7 us)
Sparse Core Ops, SparseCore 0:
  10.2 71.5 all-gather.1
